TPU v7x, 32 devices: a whole 2x2x4 slice. The times are simulated.
32 devices in a mesh: group: 2 (over y), ctx: 4 (over z), head: 2 (over x), req: 2 (over core).
Axes of the slice: x: 2, y: 2, z: 4, core: 2. Of those that a mesh axis runs over, the one named last changes fastest.
Arguments:
- fresh_hidden: bfloat16 [4, 512, 8192], P(('group', 'req'), 'ctx', 'head'), parts along dimension 0, may hold values from -6 to 6
- latent_down: bfloat16 [8192, 512], P('head'), may hold values from -0.0625 to 0.0625
- cache_latents: bfloat16 [4, 1024, 512], P(('group', 'req'), 'ctx', 'head'), parts along dimension 0, may hold values from -6 to 6
- key_up: bfloat16 [2, 256, 128], P('head'), may hold values from -0.375 to 0.375
- value_up: bfloat16 [2, 256, 128], P('head'), may hold values from -0.375 to 0.375
- queries: bfloat16 [4, 512, 2048], P(('group', 'req'), 'ctx', 'head'), parts along dimension 0, may hold values from -160 to 160
- span_start: int32 [4, 4], P(('group', 'req')), parts along dimension 0, may hold values from 0 to 3, as said below
Outputs:
- attention: bfloat16 [4, 512, 2048], P(('group', 'req'), 'ctx', 'head'), parts along dimension 0
There are 2 independent parts, one for each index of `group`. A program takes and returns all parts, laid end to end along the dimension named above; an argument that names none is the same for every part. Nothing has to cross between parts.
Inputs may be any that keep to these rules, and one draw needn't show every extreme that they name: For each request span_start is a permutation of 0 to 4 - 1 over the spans.
All inputs are finite; a program needn't handle non-finite values.
Results may differ from a plain program's by a relative error of at most 0.035.
Values may be sent and summed in bfloat16 or wider, within the bound.
No kernel may reach another device: no remote copies, remote signals or barrier semaphores. Data moves between devices by JAX's collectives and lax.ppermute only.
A program may use at most 128 MiB of HBM per device.

v0:
```python
import jax
import jax.numpy as jnp
from jax import lax
from jax.sharding import PartitionSpec as P

ROPE_BASE = 500000.0
SCORE_FLOOR = -1e30


def rotate(field, positions):
    half_dim = field.shape[-1] // 2
    inv_freq = ROPE_BASE ** (-(jnp.arange(half_dim, dtype=jnp.float32) * 2.0 / field.shape[-1]))
    angles = positions.astype(jnp.float32)[:, None] * inv_freq[None, :]
    cosine = jnp.cos(angles)
    sine_part = jnp.sin(angles)
    first_half = field[..., :half_dim]
    second_half = field[..., half_dim:]
    return jnp.concatenate(
        [
            first_half * cosine - second_half * sine_part,
            second_half * cosine + first_half * sine_part,
        ],
        axis=-1,
    )


def rebuild(latents, positions, key_up, value_up, rank_width):
    key_rows = rotate(
        jnp.dot(latents[:, :rank_width], key_up[0], preferred_element_type=jnp.float32), positions
    ).astype(jnp.bfloat16)
    value_rows = jnp.dot(
        latents[:, rank_width:], value_up[0], preferred_element_type=jnp.float32
    ).astype(jnp.bfloat16)
    return (key_rows, value_rows)


def attend(state_in, query_rows, row_pos, key_rows, value_rows, positions, score_scale):
    row_max, row_sum, weighted = state_in
    scores = (
        lax.dot_general(
            query_rows, key_rows, (((1,), (1,)), ((), ())), preferred_element_type=jnp.float32
        )
        * score_scale
    )
    visible = positions[None, :] <= row_pos[:, None]
    scores = jnp.where(visible, scores, SCORE_FLOOR)
    new_max = jnp.maximum(row_max, jnp.max(scores, axis=1))
    weights = jnp.where(visible, jnp.exp(scores - new_max[:, None]), 0.0)
    row_sum = jnp.sum(weights, axis=1)
    weighted = jnp.dot(weights.astype(jnp.bfloat16), value_rows, preferred_element_type=jnp.float32)
    return (new_max, row_sum, weighted)


def guarded(state_in, query_rows, row_pos, key_rows, value_rows, positions, score_scale):
    return attend(state_in, query_rows, row_pos, key_rows, value_rows, positions, score_scale)


def per_device(fresh_hidden, latent_down, cache_latents, key_up, value_up, queries, span_start):
    partial_value = jnp.dot(fresh_hidden[0], latent_down, preferred_element_type=jnp.float32)
    fresh_lat = lax.psum(partial_value, "head").astype(jnp.bfloat16)
    cache_full = lax.all_gather(cache_latents, "head", axis=2, tiled=True)[0]
    local_lat = jnp.concatenate([cache_full, fresh_lat], axis=0)
    tok_dev = local_lat.shape[0]
    rank_width = local_lat.shape[1] // 2
    fresh_dev = queries.shape[1]
    cache_dev = tok_dev - fresh_dev
    head_dim = key_up.shape[2]
    per_kv = queries.shape[2] // head_dim
    score_scale = head_dim ** (-0.5)
    places = span_start[0]
    span_count = places.shape[0]
    cache_total = cache_dev * span_count
    span_id = lax.axis_index("ctx")
    own_place = lax.dynamic_index_in_dim(places, span_id, keepdims=False)
    query_pos = cache_total + own_place * fresh_dev + jnp.arange(fresh_dev, dtype=jnp.int32)
    cache_pos = places[:, None] * cache_dev + jnp.arange(cache_dev, dtype=jnp.int32)[None, :]
    fresh_pos = (
        cache_total + places[:, None] * fresh_dev + jnp.arange(fresh_dev, dtype=jnp.int32)[None, :]
    )
    key_pos_all = jnp.concatenate([cache_pos, fresh_pos], axis=1).reshape(-1)
    query_heads = (
        queries[0].reshape(fresh_dev, per_kv, head_dim).transpose(1, 0, 2).astype(jnp.float32)
    )
    query_rows = (
        rotate(query_heads, query_pos).astype(jnp.bfloat16).reshape(per_kv * fresh_dev, head_dim)
    )
    row_pos = jnp.tile(query_pos, per_kv)
    row_count = per_kv * fresh_dev
    initial = (
        jnp.full((row_count,), SCORE_FLOOR, jnp.float32),
        jnp.zeros((row_count,), jnp.float32),
        jnp.zeros((row_count, head_dim), jnp.float32),
    )
    own_pos = lax.dynamic_slice_in_dim(key_pos_all, span_id * tok_dev, tok_dev)
    own_keys, own_values = rebuild(local_lat, own_pos, key_up, value_up, rank_width)
    state = guarded(
        initial,
        query_rows,
        row_pos,
        lax.all_gather(own_keys, "ctx", axis=0, tiled=True),
        lax.all_gather(own_values, "ctx", axis=0, tiled=True),
        key_pos_all,
        score_scale,
    )
    row_max, row_sum, weighted = state
    mixed = (weighted / row_sum[:, None]).astype(jnp.bfloat16)
    mixed = (
        mixed.reshape(per_kv, fresh_dev, head_dim)
        .transpose(1, 0, 2)
        .reshape(1, fresh_dev, per_kv * head_dim)
    )
    return mixed


def solution(mesh):
    return jax.shard_map(
        per_device,
        mesh=mesh,
        in_specs=(
            P(("group", "req"), "ctx", "head"),
            P("head", None),
            P(("group", "req"), "ctx", "head"),
            P("head", None, None),
            P("head", None, None),
            P(("group", "req"), "ctx", "head"),
            P(("group", "req"), None),
        ),
        out_specs=P(("group", "req"), "ctx", "head"),
        check_vma=False,
    )
```

profile of v0, /device:TPU:0, one launch (start us, length us, event | category | flops | bytes accessed | tf_op | source)
XLA Modules:
  0.0 63.9 jit_solution(10641969654796852829)
XLA Ops:
  0.0 0.0 copy-start
  0.0 1.3 %fusion.38 = s32[1,1]{1,0:T(1,128)} fusion(s32[1,4]{1,0:T(1,128)} %param.13, s32[]{:T(128)S(6)} %select_n.14), kind=kLoop, calls=%fused_computation.59 | loop fusion | flops 1 | bytes 12 | tf_op jit(solution)/shard_map/mul | solution.py:75
  2.1 0.7 %multiply_bitcast_fusion = (s32[4]{0:T(128)S(1)}, s32[4]{0:T(128)S(1)}) fusion(s32[1,4]{1,0:T(1,128)} %param.13), kind=kLoop, calls=%fused_computation.50 | loop fusion | flops 12 | bytes 48 | tf_op jit(solution)/shard_map/mul | solution.py:76
  2.7 0.1 iota_add_fusion.1
  2.8 0.1 iota_add_fusion
  2.9 0.1 dynamic-slice_convert_fusion
  3.0 0.2 multiply_cosine_fusion.1
  3.2 0.0 copy-done
  3.2 2.9 %fusion.5 = f32[128,512]{1,0:T(8,128)S(1)} fusion(bf16[4096,512]{1,0:T(8,128)(2,1)} %param.8, bf16[1,128,4096]{2,1,0:T(8,128)(2,1)S(1)} %copy-done), kind=kOutput, calls=%fused_computation.7 | convolution fusion | flops 536870912 | bytes 5505024 | tf_op jit(solution)/shard_map/dot_general | solution.py:59
  6.1 13.0 %all-reduce.1 = bf16[128,512]{1,0:T(8,128)(2,1)S(1)} all-reduce(f32[128,512]{1,0:T(8,128)S(1)} %fusion.5), channel_id=1, replica_groups=mesh['group'=2,'ctx'=4,'head'=2,'req'=2] {'head'}, use_global_device_ids=true, to_apply=%region_0.0 | all-reduce | flops 65536 | bytes 393216 | tf_op jit(solution)/shard_map/psum | solution.py:60
  19.1 5.8 %all_gather.9 = bf16[1,256,512]{2,1,0:T(8,128)(2,1)S(1)} all-gather(bf16[1,256,256]{2,1,0:T(8,128)(2,1)} %param.9), channel_id=1, replica_groups=mesh['group'=2,'ctx'=4,'head'=2,'req'=2] {'head'}, dimensions={2}, use_global_device_ids=true | all-gather | bytes 393216 | tf_op jit(solution)/shard_map/all_gather | solution.py:61
  24.9 0.2 convolution_convert_fusion
  25.2 0.2 fusion.18
  25.4 0.4 fusion.26
  25.9 15.7 %all_gather.10 = bf16[1536,128]{0,1:T(8,128)(2,1)S(1)} all-gather(bf16[384,128]{0,1:T(8,128)(2,1)S(1)} %pad_maximum_fusion.2), channel_id=1, replica_groups=mesh['group'=2,'ctx'=4,'head'=2,'req'=2] {'ctx'}, dimensions={0}, use_global_device_ids=true | all-gather | bytes 491520 | tf_op jit(solution)/shard_map/all_gather | solution.py:100
  41.5 15.0 %all_gather.11 = bf16[1536,128]{1,0:T(8,128)(2,1)S(1)} all-gather(bf16[384,128]{1,0:T(8,128)(2,1)S(1)} %convolution_convert_fusion), channel_id=1, replica_groups=mesh['group'=2,'ctx'=4,'head'=2,'req'=2] {'ctx'}, dimensions={0}, use_global_device_ids=true | all-gather | bytes 491520 | tf_op jit(solution)/shard_map/all_gather | solution.py:101
  56.6 0.1 copy.11
  56.7 0.3 copy.9
  57.0 0.1 subtract_convert_fusion
  57.1 1.3 %fusion = (f32[1024]{0:T(1024)S(1)}, f32[1024,1536]{1,0:T(8,128)S(1)}) fusion(s32[1536]{0:T(1024)S(1)} %le.17, s32[1024]{0:T(1024)S(1)} %broadcast_bitcast_fusion, bf16[1536,128]{0,1:T(8,128)(2,1)S(1)} %all_gather.10, bf16[1024,64]{0,1:T(8,128)(2,1)S(1)} %get-tuple-element.15, bf16[1024,64]{0,1:T(8,128)(2,1)S(1)} %get-tuple-element.16), kind=kOutput, calls=%fused_computation.2 | convolution fusion | flops 409467904 | bytes 6961152 | tf_op jit(solution)/shard_map/dot_general | solution.py:40
  58.4 2.3 %fusion.1 = f32[1024]{0:T(1024)S(1)} fusion(f32[1024,1536]{1,0:T(8,128)S(1)} %get-tuple-element.14, f32[1024]{0:T(1024)S(1)} %broadcast_maximum_fusion, s32[1536]{0:T(1024)S(1)} %le.17, s32[1024]{0:T(1024)S(1)} %broadcast_bitcast_fusion), kind=kLoop, calls=%fused_computation.3 | loop fusion | flops 9436160 | bytes 6309888 | tf_op jit(solution)/shard_map/reduce_sum | solution.py:49
  60.7 2.1 %fusion.10 = bf16[1024,128]{1,0:T(8,128)(2,1)S(1)} fusion(bf16[1536,128]{1,0:T(8,128)(2,1)S(1)} %all_gather.11, f32[1024,1536]{1,0:T(8,128)S(1)} %get-tuple-element.14, f32[1024]{0:T(1024)S(1)} %broadcast_maximum_fusion, s32[1536]{0:T(1024)S(1)} %le.17, s32[1024]{0:T(1024)S(1)} %broadcast_bitcast_fusion, f32[1024]{0:T(1024)S(1)} %fusion.1), kind=kOutput, calls=%fused_computation.10 | convolution fusion | flops 412352512 | bytes 6965248 | tf_op jit(solution)/shard_map/dot_general | solution.py:50
  62.9 0.2 copy.10
  63.0 0.8 %reshape.120 = bf16[1,128,1024]{2,1,0:T(8,128)(2,1)} reshape(bf16[128,8,128]{2,1,0:T(8,128)(2,1)S(1)} %copy.10) | data formatting | bytes 524288 | tf_op jit(solution)/shard_map/reshape | solution.py:110
  (16 shorter events, 0.1 us)
Async XLA Ops:
  0.0 3.2 %copy-start = (bf16[1,128,4096]{2,1,0:T(8,128)(2,1)S(1)}, bf16[1,128,4096]{2,1,0:T(8,128)(2,1)}, u32[]{:S(2)}) copy-start(bf16[1,128,4096]{2,1,0:T(8,128)(2,1)} %param.7) | copy-start | bytes 3145732
  0.0 56.5 %copy-start.1 = (bf16[1,128,1024]{2,1,0:T(8,128)(2,1)S(1)}, bf16[1,128,1024]{2,1,0:T(8,128)(2,1)}, u32[]{:S(2)}) copy-start(bf16[1,128,1024]{2,1,0:T(8,128)(2,1)} %param.12) | copy-start | bytes 786436
  0.0 24.9 %copy-start.2 = (bf16[1,256,128]{2,1,0:T(8,128)(2,1)S(1)}, bf16[1,256,128]{2,1,0:T(8,128)(2,1)}, u32[]{:S(2)}) copy-start(bf16[1,256,128]{2,1,0:T(8,128)(2,1)} %param.11) | copy-start | bytes 196612
  0.0 25.2 %copy-start.3 = (bf16[1,256,128]{2,1,0:T(8,128)(2,1)S(1)}, bf16[1,256,128]{2,1,0:T(8,128)(2,1)}, u32[]{:S(2)}) copy-start(bf16[1,256,128]{2,1,0:T(8,128)(2,1)} %param.10) | copy-start | bytes 196612
where the time goes:
time: 64.1 us; the launch traced here: 63.9 us
  blocking collectives  49.5 us (77%)
  matrix products  6.79 us (11%)
  other arithmetic  5.33 us (8%)
  local copies, waits for them, and re-layouts  1.42 us (2%)
  between operations  0.81 us (1%)
    all_gather x1, blocking collectives, per_device(): lax.all_gather(own_keys, 'ctx', axis=0, tiled=True)  15.7 us
    all_gather x1, blocking collectives, per_device(): lax.all_gather(own_values, 'ctx', axis=0, tiled=True)  15 us
    psum x1, blocking collectives, per_device(): fresh_lat = lax.psum(partial_value, 'head').astype(jnp.bfloat16)  13 us
    all_gather x1, blocking collectives, per_device(): cache_full = lax.all_gather(cache_latents, 'head', axis=2, tiled=True)[0]  5.85 us
    dot_general x1, matrix products, per_device(): jnp.dot(fresh_hidden[0], latent_down, preferred_element_type=jnp.float32)  2.9 us
    reduce_sum x1, other arithmetic, attend(): row_sum = jnp.sum(weights, axis=1)  2.29 us
    dot_general x1, matrix products, attend(): jnp.dot(weights.astype(jnp.bfloat16), value_rows, preferred_element_type=...  2.12 us
    mul x1, other arithmetic, per_device(): own_place * fresh_dev  1.35 us

commit v1 on v0

--- a/solution.py
+++ b/solution.py
@@ -57,7 +57,7 @@
 
 def per_device(fresh_hidden, latent_down, cache_latents, key_up, value_up, queries, span_start):
     partial_value = jnp.dot(fresh_hidden[0], latent_down, preferred_element_type=jnp.float32)
-    fresh_lat = lax.psum(partial_value, "head").astype(jnp.bfloat16)
+    fresh_lat = jnp.sum(lax.all_gather(partial_value, "head"), axis=0).astype(jnp.bfloat16)
     cache_full = lax.all_gather(cache_latents, "head", axis=2, tiled=True)[0]
     local_lat = jnp.concatenate([cache_full, fresh_lat], axis=0)
     tok_dev = local_lat.shape[0]

time: 64.1 us -> 60.8 us (0.949)
  blocking collectives: 49.5 us -> 46.1 us
    psum x1 -> x0, blocking collectives: 13 us -> none  [per_device(): fresh_lat = lax.psum(partial_value, 'head').astype(jnp.bfloat16)]
    all_gather x0 -> x1, blocking collectives: none -> 9.94 us  [per_device(): lax.all_gather(partial_value, 'head')]
where the time goes in v1:
time: 60.8 us; the launch traced here: 60.6 us
  blocking collectives  46.1 us (76%)
  matrix products  6.78 us (11%)
  other arithmetic  5.4 us (9%)
  local copies, waits for them, and re-layouts  1.42 us (2%)
  between operations  0.83 us (1%)
    all_gather x1, blocking collectives, per_device(): lax.all_gather(own_keys, 'ctx', axis=0, tiled=True)  15.5 us
    all_gather x1, blocking collectives, per_device(): lax.all_gather(own_values, 'ctx', axis=0, tiled=True)  15.1 us
    all_gather x1, blocking collectives, per_device(): lax.all_gather(partial_value, 'head')  9.94 us
    all_gather x1, blocking collectives, per_device(): cache_full = lax.all_gather(cache_latents, 'head', axis=2, tiled=True)[0]  5.64 us
    dot_general x1, matrix products, per_device(): jnp.dot(fresh_hidden[0], latent_down, preferred_element_type=jnp.float32)  2.9 us
    reduce_sum x1, other arithmetic, attend(): row_sum = jnp.sum(weights, axis=1)  2.29 us
    dot_general x1, matrix products, attend(): jnp.dot(weights.astype(jnp.bfloat16), value_rows, preferred_element_type=...  2.12 us
    mul x1, other arithmetic, per_device(): own_place * fresh_dev  1.39 us

profile of v1, /device:TPU:0, one launch (start us, length us, event | category | flops | bytes accessed | tf_op | source)
XLA Modules:
  0.0 60.6 jit_solution(12137452192393633494)
XLA Ops:
  0.0 0.0 copy-start
  0.0 0.0 copy-start.2
  0.0 1.4 %fusion.38 = s32[1,1]{1,0:T(1,128)} fusion(s32[1,4]{1,0:T(1,128)} %param.13, s32[]{:T(128)S(6)} %select_n.14), kind=kLoop, calls=%fused_computation.59 | loop fusion | flops 1 | bytes 12 | tf_op jit(solution)/shard_map/mul | solution.py:75
  2.1 0.7 %multiply_bitcast_fusion = (s32[4]{0:T(128)S(1)}, s32[4]{0:T(128)S(1)}) fusion(s32[1,4]{1,0:T(1,128)} %param.13), kind=kLoop, calls=%fused_computation.50 | loop fusion | flops 12 | bytes 48 | tf_op jit(solution)/shard_map/mul | solution.py:76
  2.8 0.1 iota_add_fusion.1
  2.9 0.1 iota_add_fusion
  2.9 0.1 dynamic-slice_convert_fusion
  3.0 0.2 multiply_cosine_fusion.1
  3.2 2.9 %fusion.5 = f32[128,512]{1,0:T(8,128)S(1)} fusion(bf16[4096,512]{1,0:T(8,128)(2,1)} %param.8, bf16[1,128,4096]{2,1,0:T(8,128)(2,1)S(1)} %copy-done), kind=kOutput, calls=%fused_computation.7 | convolution fusion | flops 536870912 | bytes 5505024 | tf_op jit(solution)/shard_map/dot_general | solution.py:59
  6.1 9.9 %all-gather = f32[256,512]{1,0:T(8,128)S(1)} all-gather(f32[128,512]{1,0:T(8,128)S(1)} %fusion.5), channel_id=2, replica_groups=mesh['group'=2,'ctx'=4,'head'=2,'req'=2] {'head'}, dimensions={0}, use_global_device_ids=true | all-gather | bytes 786432 | tf_op jit(solution)/shard_map/all_gather | solution.py:60
  16.1 5.6 %all_gather.15 = bf16[1,256,512]{2,1,0:T(8,128)(2,1)S(1)} all-gather(bf16[1,256,256]{2,1,0:T(8,128)(2,1)S(1)} %copy-done.2), channel_id=1, replica_groups=mesh['group'=2,'ctx'=4,'head'=2,'req'=2] {'head'}, dimensions={2}, use_global_device_ids=true | all-gather | bytes 393216 | tf_op jit(solution)/shard_map/all_gather | solution.py:61
  21.8 0.2 convolution_convert_fusion
  22.0 0.2 fusion.18
  22.2 0.4 fusion.26
  22.7 15.5 %all_gather.18 = bf16[1536,128]{0,1:T(8,128)(2,1)S(1)} all-gather(bf16[384,128]{0,1:T(8,128)(2,1)S(1)} %pad_maximum_fusion.2), channel_id=1, replica_groups=mesh['group'=2,'ctx'=4,'head'=2,'req'=2] {'ctx'}, dimensions={0}, use_global_device_ids=true | all-gather | bytes 491520 | tf_op jit(solution)/shard_map/all_gather | solution.py:100
  38.2 15.1 %all_gather.19 = bf16[1536,128]{1,0:T(8,128)(2,1)S(1)} all-gather(bf16[384,128]{1,0:T(8,128)(2,1)S(1)} %convolution_convert_fusion), channel_id=1, replica_groups=mesh['group'=2,'ctx'=4,'head'=2,'req'=2] {'ctx'}, dimensions={0}, use_global_device_ids=true | all-gather | bytes 491520 | tf_op jit(solution)/shard_map/all_gather | solution.py:101
  53.3 0.1 copy.11
  53.4 0.3 copy.9
  53.7 0.1 subtract_convert_fusion
  53.8 1.3 %fusion = (f32[1024]{0:T(1024)S(1)}, f32[1024,1536]{1,0:T(8,128)S(1)}) fusion(s32[1536]{0:T(1024)S(1)} %le.17, s32[1024]{0:T(1024)S(1)} %broadcast_bitcast_fusion, bf16[1536,128]{0,1:T(8,128)(2,1)S(1)} %all_gather.18, bf16[1024,64]{0,1:T(8,128)(2,1)S(1)} %get-tuple-element.15, bf16[1024,64]{0,1:T(8,128)(2,1)S(1)} %get-tuple-element.16), kind=kOutput, calls=%fused_computation.2 | convolution fusion | flops 409467904 | bytes 6961152 | tf_op jit(solution)/shard_map/dot_general | solution.py:40
  55.1 2.3 %fusion.1 = f32[1024]{0:T(1024)S(1)} fusion(f32[1024,1536]{1,0:T(8,128)S(1)} %get-tuple-element.14, f32[1024]{0:T(1024)S(1)} %broadcast_maximum_fusion, s32[1536]{0:T(1024)S(1)} %le.17, s32[1024]{0:T(1024)S(1)} %broadcast_bitcast_fusion), kind=kLoop, calls=%fused_computation.3 | loop fusion | flops 9436160 | bytes 6309888 | tf_op jit(solution)/shard_map/reduce_sum | solution.py:49
  57.4 2.1 %fusion.10 = bf16[1024,128]{1,0:T(8,128)(2,1)S(1)} fusion(bf16[1536,128]{1,0:T(8,128)(2,1)S(1)} %all_gather.19, f32[1024,1536]{1,0:T(8,128)S(1)} %get-tuple-element.14, f32[1024]{0:T(1024)S(1)} %broadcast_maximum_fusion, s32[1536]{0:T(1024)S(1)} %le.17, s32[1024]{0:T(1024)S(1)} %broadcast_bitcast_fusion, f32[1024]{0:T(1024)S(1)} %fusion.1), kind=kOutput, calls=%fused_computation.10 | convolution fusion | flops 412352512 | bytes 6965248 | tf_op jit(solution)/shard_map/dot_general | solution.py:50
  59.6 0.2 copy.10
  59.7 0.8 %reshape.120 = bf16[1,128,1024]{2,1,0:T(8,128)(2,1)} reshape(bf16[128,8,128]{2,1,0:T(8,128)(2,1)S(1)} %copy.10) | data formatting | bytes 524288 | tf_op jit(solution)/shard_map/reshape | solution.py:110
  (19 shorter events, 0.2 us)
Async XLA Ops:
  0.0 3.2 %copy-start = (bf16[1,128,4096]{2,1,0:T(8,128)(2,1)S(1)}, bf16[1,128,4096]{2,1,0:T(8,128)(2,1)}, u32[]{:S(2)}) copy-start(bf16[1,128,4096]{2,1,0:T(8,128)(2,1)} %param.7) | copy-start | bytes 3145732
  0.0 53.2 %copy-start.1 = (bf16[1,128,1024]{2,1,0:T(8,128)(2,1)S(1)}, bf16[1,128,1024]{2,1,0:T(8,128)(2,1)}, u32[]{:S(2)}) copy-start(bf16[1,128,1024]{2,1,0:T(8,128)(2,1)} %param.12) | copy-start | bytes 786436
  0.0 21.8 %copy-start.3 = (bf16[1,256,128]{2,1,0:T(8,128)(2,1)S(1)}, bf16[1,256,128]{2,1,0:T(8,128)(2,1)}, u32[]{:S(2)}) copy-start(bf16[1,256,128]{2,1,0:T(8,128)(2,1)} %param.11) | copy-start | bytes 196612
  0.0 22.0 %copy-start.4 = (bf16[1,256,128]{2,1,0:T(8,128)(2,1)S(1)}, bf16[1,256,128]{2,1,0:T(8,128)(2,1)}, u32[]{:S(2)}) copy-start(bf16[1,256,128]{2,1,0:T(8,128)(2,1)} %param.10) | copy-start | bytes 196612
  0.0 16.1 %copy-start.2 = (bf16[1,256,256]{2,1,0:T(8,128)(2,1)S(1)}, bf16[1,256,256]{2,1,0:T(8,128)(2,1)}, u32[]{:S(2)}) copy-start(bf16[1,256,256]{2,1,0:T(8,128)(2,1)} %param.9) | copy-start | bytes 393220
